TPU v7x, 32 devices: a whole 2x2x4 slice. The times are simulated.
32 devices in a mesh: dp: 8 (over z, y), tensor: 4 (over x, core).
Axes of the slice: x: 2, y: 2, z: 4, core: 2. Of those that a mesh axis runs over, the one named last changes fastest.
Arguments:
- layer_outs: bfloat16 [5, 8192, 4096], P(None, 'dp', 'tensor'), may hold values from -6 to 6
- avg_grads: bfloat16 [4, 8192, 4096], P(None, 'dp', 'tensor'), may hold values from -0.0010299683 to 0.0010299683
- attn_mixed: bfloat16 [8192, 4096], P('dp', 'tensor'), may hold values from -96 to 96
- dwa_coefs: float32 [4, 5], replicated, may hold values from -1.5 to 1.5
Outputs:
- coef_grad: float32 [4, 5], replicated
- proj_grad: float32 [4096, 4096], P('dp', 'tensor')
All inputs are finite; a program needn't handle non-finite values.
Results may differ from a plain program's by a relative error of at most 0.0042.
Values may be sent and summed in bfloat16 or wider, within the bound.
A program may use at most 128 MiB of HBM per device.

v0:
```python
import functools

import jax
import jax.numpy as jnp
from jax import lax
from jax.experimental import pallas as pl
from jax.experimental.pallas import tpu as pltpu
from jax.sharding import PartitionSpec as P

CHUNKS = 8
GROUP = 4
LANES = 128


def kernel(
    dp_size, tensor_size, outs_hbm, grads_hbm, attn_hbm, coefs, coef_out, proj_out,
    outs, grads, attn, gathered, y_send, y_recv, own, z_left, z_right, coef_a, coef_b,
    load_sem, g_send, x_send, g_recv, y_send_sem, y_recv_sem,
    z_send_sem, zl_sem, zr_sem, ca_send, ca_recv, cb_send, cb_recv,
):
    depth, tokens, features = grads.shape
    rows, cols = proj_out.shape
    ys = dp_size // tensor_size
    zs = tensor_size
    xs = tensor_size // 2
    chunk = rows // CHUNKS
    dp, tensor = lax.axis_index("dp"), lax.axis_index("tensor")
    z, y = dp // ys, dp % ys
    x, core = tensor // 2, tensor % 2
    partner = x * 2 + 1 - core

    loads = []
    order = [depth - 2, depth - 1]
    for i in order:
        loads.append(pltpu.make_async_copy(grads_hbm.at[i], grads.at[i], load_sem.at[i]))
    loads.append(pltpu.make_async_copy(attn_hbm, attn, load_sem.at[depth]))
    for i in range(depth - 2):
        loads.append(pltpu.make_async_copy(grads_hbm.at[i], grads.at[i], load_sem.at[i]))
    for j in range(depth + 1):
        loads.append(pltpu.make_async_copy(outs_hbm.at[j], outs.at[j], load_sem.at[depth + 1 + j]))
    for load in loads[:3]:
        load.start()

    barrier = pltpu.get_barrier_semaphore()
    for i in range(1, tensor_size):
        pl.semaphore_signal(
            barrier, inc=1, device_id={"tensor": (tensor + i) % tensor_size},
            device_id_type=pl.DeviceIdType.MESH,
        )
    for i in range(1, dp_size):
        pl.semaphore_signal(
            barrier, inc=1, device_id={"dp": (dp + i) % dp_size},
            device_id_type=pl.DeviceIdType.MESH,
        )
    pl.semaphore_wait(barrier, tensor_size + dp_size - 2)

    def piece(slot, part):
        return gathered.at[slot, pl.ds(pl.multiple_of(part * rows, rows), rows), :]

    def to_partner(slot, part):
        return pltpu.make_async_remote_copy(
            src_ref=piece(slot, part), dst_ref=piece(slot, part),
            send_sem=g_send.at[slot // 2, part], recv_sem=g_recv.at[slot, part],
            device_id={"tensor": partner}, device_id_type=pl.DeviceIdType.MESH,
        )

    def to_x(other, part):
        return pltpu.make_async_remote_copy(
            src_ref=piece(tensor, part), dst_ref=piece(tensor, part),
            send_sem=x_send.at[other, part], recv_sem=g_recv.at[tensor, part],
            device_id={"tensor": other * 2 + core}, device_id_type=pl.DeviceIdType.MESH,
        )

    def arrive(slot, part):
        pltpu.make_async_remote_copy(
            src_ref=piece(slot, part), dst_ref=piece(slot, part),
            send_sem=g_send.at[slot // 2, part], recv_sem=g_recv.at[slot, part],
            device_id={"tensor": partner}, device_id_type=pl.DeviceIdType.MESH,
        ).wait_recv()

    def make(part):
        first, second = coefs[depth - 2, depth - 1], coefs[depth - 1, depth - 1]

        @pl.loop(0, tokens // LANES)
        def _(step):
            at = pl.ds(pl.multiple_of(step * LANES, LANES), LANES)
            wide = pl.ds(pl.multiple_of(part * rows, LANES), rows)
            value = first * grads[depth - 2, at, wide].astype(jnp.float32)
            value += second * grads[depth - 1, at, wide].astype(jnp.float32)
            into = pl.ds(pl.multiple_of(part * rows, rows), rows)
            gathered[tensor, into, at] = value.T.astype(jnp.bfloat16)

        to_partner(tensor, part).start()
        for i in range(1, xs):
            to_x((x + i) % xs, part).start()

    def block(slot, part, k):
        at = pl.ds(pl.multiple_of(part * rows + k * chunk, chunk), chunk * GROUP)
        return jnp.dot(gathered[slot, at, :], attn[...], preferred_element_type=jnp.float32)

    def strip(k, count=1):
        return pl.ds(pl.multiple_of(k * chunk, chunk), chunk * count)

    def y_copy(slot, i, k):
        return pltpu.make_async_remote_copy(
            src_ref=y_send.at[i - 1, slot, strip(k), :], dst_ref=y_recv.at[i - 1, slot, strip(k), :],
            send_sem=y_send_sem.at[i - 1, slot, k], recv_sem=y_recv_sem.at[i - 1, slot, k],
            device_id={"dp": z * ys + (y + i) % ys}, device_id_type=pl.DeviceIdType.MESH,
        )

    def y_start(slot):
        for i in range(1, ys):
            @pl.loop(0, CHUNKS // GROUP)
            def _(g):
                k = g * GROUP
                value = block(slot, (y + i) % ys, k)
                y_send[i - 1, slot, strip(k, GROUP), :] = value.astype(jnp.bfloat16)
                for n in range(GROUP):
                    y_copy(slot, i, k + n).start()

    def keep(slot):
        @pl.loop(0, CHUNKS // GROUP)
        def _(g):
            k = g * GROUP
            own[slot, strip(k, GROUP), :] = block(slot, y, k)

    def right_copy(slot, k):
        return pltpu.make_async_remote_copy(
            src_ref=y_send.at[0, slot, strip(k), :], dst_ref=z_left.at[slot, strip(k), :],
            send_sem=z_send_sem.at[slot, k], recv_sem=zl_sem.at[slot, k],
            device_id={"dp": dp + ys}, device_id_type=pl.DeviceIdType.MESH,
        )

    def left_copy(slot, k):
        return pltpu.make_async_remote_copy(
            src_ref=y_send.at[0, slot, strip(k), :], dst_ref=z_right.at[slot, strip(k), :],
            send_sem=z_send_sem.at[slot, k], recv_sem=zr_sem.at[slot, k],
            device_id={"dp": dp - ys}, device_id_type=pl.DeviceIdType.MESH,
        )

    def pass_on(slot):
        @pl.loop(0, CHUNKS)
        def _(k):
            total = own[slot, strip(k), :]
            for i in range(1, ys):
                y_copy(slot, i, k).wait_send()
                y_copy(slot, i, k).wait_recv()
                total += y_recv[i - 1, slot, strip(k), :].astype(jnp.float32)
            own[slot, strip(k), :] = total

            @pl.when(slot > z)
            def _():
                @pl.when(z > 0)
                def _():
                    right_copy(slot, k).wait_recv()
                    own[slot, strip(k), :] += z_left[slot, strip(k), :].astype(jnp.float32)

                y_send[0, slot, strip(k), :] = own[slot, strip(k), :].astype(jnp.bfloat16)
                right_copy(slot, k).start()

            @pl.when(slot < z)
            def _():
                @pl.when(z < zs - 1)
                def _():
                    left_copy(slot, k).wait_recv()
                    own[slot, strip(k), :] += z_right[slot, strip(k), :].astype(jnp.float32)

                y_send[0, slot, strip(k), :] = own[slot, strip(k), :].astype(jnp.bfloat16)
                left_copy(slot, k).start()

    def coef_partial():
        pairs = [(i, j) for i in range(depth) for j in range(min(i + 2, depth + 1))]

        def step(r, sums):
            at = pl.ds(pl.multiple_of(r * 16, 16), 16)
            sums = list(sums)
            for col in range(features // LANES):
                lanes = slice(col * LANES, (col + 1) * LANES)
                g = [grads[i, at, lanes].astype(jnp.float32) for i in range(depth)]
                o = [outs[j, at, lanes].astype(jnp.float32) for j in range(depth + 1)]
                for n, (i, j) in enumerate(pairs):
                    product = g[i] * o[j]
                    sums[n] += product[:8] + product[8:]
            return tuple(sums)

        zero = jnp.zeros((8, LANES), jnp.float32)
        sums = lax.fori_loop(0, tokens // 16, step, tuple(zero for _ in pairs))
        row = lax.broadcasted_iota(jnp.int32, (8, LANES), 0)
        col = lax.broadcasted_iota(jnp.int32, (8, LANES), 1)
        tile = zero
        for n, (i, j) in enumerate(pairs):
            value = jnp.sum(sums[n], axis=(0, 1), keepdims=True)
            tile = jnp.where((row == i) & (col == j), value, tile)
        return tile

    def a_copy(i, slot):
        return pltpu.make_async_remote_copy(
            src_ref=coef_a.at[slot], dst_ref=coef_a.at[slot],
            send_sem=ca_send.at[i], recv_sem=ca_recv.at[slot],
            device_id={"tensor": (tensor + i) % tensor_size},
            device_id_type=pl.DeviceIdType.MESH,
        )

    def b_copy(i, slot):
        return pltpu.make_async_remote_copy(
            src_ref=coef_b.at[slot], dst_ref=coef_b.at[slot],
            send_sem=cb_send.at[i], recv_sem=cb_recv.at[slot],
            device_id={"dp": (dp + i) % dp_size}, device_id_type=pl.DeviceIdType.MESH,
        )

    loads[0].wait()
    loads[1].wait()
    for i in range(1, ys):
        make((y + i) % ys)
    loads[2].wait()
    y_start(tensor)
    for load in loads[3:]:
        load.start()
    make(y)
    for i in range(1, ys):
        arrive(partner, (y + i) % ys)
    y_start(partner)
    keep(tensor)
    arrive(partner, y)
    keep(partner)

    for load in loads[3:]:
        load.wait()
    coef_a[tensor] = coef_partial()
    for i in range(1, tensor_size):
        a_copy(i, tensor).start()

    others = []
    for n in range(1, xs):
        other = (x + n) % xs
        far = jnp.where(other < xs // 2, other * 2, other * 2 + 1)
        others.append((other, far, other * 4 + 1 - far))

    for other, far, near in others:
        for i in range(1, ys):
            arrive(other * 2 + core, (y + i) % ys)
            to_partner(other * 2 + core, (y + i) % ys).start()
        for i in range(1, ys):
            arrive(other * 2 + 1 - core, (y + i) % ys)
        y_start(far)
        y_start(near)

    pass_on(tensor)
    for i in range(1, tensor_size):
        a_copy(i, (tensor + tensor_size - i) % tensor_size).wait_recv()
    total = coef_a[0]
    for i in range(1, tensor_size):
        total += coef_a[i]
    coef_b[dp] = total
    for i in range(1, dp_size):
        b_copy(i, dp).start()

    for other, far, near in others:
        arrive(other * 2 + core, y)
        to_partner(other * 2 + core, y).start()
        arrive(other * 2 + 1 - core, y)
        keep(far)
        keep(near)
    pass_on(partner)
    for other, far, near in others:
        pass_on(far)
        pass_on(near)

    for i in range(1, dp_size):
        b_copy(i, (dp + dp_size - i) % dp_size).wait_recv()
    total = coef_b[0]
    for i in range(1, dp_size):
        total += coef_b[i]
    coef_out[...] = total[: coef_out.shape[0], : coef_out.shape[1]]

    @pl.loop(0, CHUNKS)
    def _(k):
        proj_out[strip(k), :] = own[z, strip(k), :]

        @pl.when(z > 0)
        def _():
            right_copy(z, k).wait_recv()
            proj_out[strip(k), :] += z_left[z, strip(k), :].astype(jnp.float32)

        @pl.when(z < zs - 1)
        def _():
            left_copy(z, k).wait_recv()
            proj_out[strip(k), :] += z_right[z, strip(k), :].astype(jnp.float32)

    for slot in range(zs):
        @pl.when(slot != z)
        def _():
            @pl.loop(0, CHUNKS)
            def _(k):
                right_copy(slot, k).wait_send()

    for part in range(ys):
        for n in range(xs):
            to_partner(n * 2 + core, part).wait_send()
        for n in range(1, xs):
            to_x((x + n) % xs, part).wait_send()
    for i in range(1, tensor_size):
        a_copy(i, tensor).wait_send()
    for i in range(1, dp_size):
        b_copy(i, dp).wait_send()


def local(dp_size, tensor_size, layer_outs, avg_grads, attn_mixed, dwa_coefs):
    depth, tokens, features = avg_grads.shape
    rows = features * tensor_size // dp_size
    cols = attn_mixed.shape[1]
    ys, zs, xs = dp_size // tensor_size, tensor_size, tensor_size // 2
    bf16, f32 = jnp.bfloat16, jnp.float32
    dma = pltpu.SemaphoreType.DMA
    any_space = pl.BlockSpec(memory_space=pl.ANY)
    vmem = pl.BlockSpec(memory_space=pltpu.VMEM)
    return pl.pallas_call(
        functools.partial(kernel, dp_size, tensor_size),
        out_shape=(
            jax.ShapeDtypeStruct(dwa_coefs.shape, f32),
            jax.ShapeDtypeStruct((rows, cols), f32),
        ),
        in_specs=[any_space, any_space, any_space, pl.BlockSpec(memory_space=pltpu.SMEM)],
        out_specs=(vmem, vmem),
        scratch_shapes=[
            pltpu.VMEM(layer_outs.shape, bf16),
            pltpu.VMEM(avg_grads.shape, bf16),
            pltpu.VMEM(attn_mixed.shape, bf16),
            pltpu.VMEM((tensor_size, features, tokens), bf16),
            pltpu.VMEM((ys - 1, zs, rows, cols), bf16),
            pltpu.VMEM((ys - 1, zs, rows, cols), bf16),
            pltpu.VMEM((zs, rows, cols), f32),
            pltpu.VMEM((zs, rows, cols), bf16),
            pltpu.VMEM((zs, rows, cols), bf16),
            pltpu.VMEM((tensor_size, 8, LANES), f32),
            pltpu.VMEM((dp_size, 8, LANES), f32),
            dma((2 * depth + 2,)),
            dma((xs, ys)),
            dma((xs, ys)),
            dma((tensor_size, ys)),
            dma((ys - 1, zs, CHUNKS)),
            dma((ys - 1, zs, CHUNKS)),
            dma((zs, CHUNKS)),
            dma((zs, CHUNKS)),
            dma((zs, CHUNKS)),
            dma((tensor_size,)),
            dma((tensor_size,)),
            dma((dp_size,)),
            dma((dp_size,)),
        ],
        compiler_params=pltpu.CompilerParams(
            collective_id=0, has_side_effects=True, vmem_limit_bytes=67000000
        ),
    )(layer_outs, avg_grads, attn_mixed, dwa_coefs)


def solution(mesh):
    sizes = (mesh.shape["dp"], mesh.shape["tensor"])
    in_specs = (P(None, "dp", "tensor"), P(None, "dp", "tensor"), P("dp", "tensor"), P())
    out_specs = (P(), P("dp", "tensor"))
    return jax.shard_map(
        functools.partial(local, *sizes), mesh=mesh, in_specs=in_specs, out_specs=out_specs, check_vma=False
    )
```

profile of v0, /device:TPU:17, one launch (start us, length us, event | category | flops | bytes accessed | tf_op | source)
XLA Modules:
  0.0 141.4 jit_solution(8759425307819209105)
XLA Ops:
  0.6 136.4 %shard_map.59 = (f32[4,5]{1,0:T(4,128)}, f32[512,1024]{1,0:T(8,128)}) custom-call(bf16[5,1024,1024]{2,1,0:T(8,128)(2,1)} %outs_hbm.1, bf16[4,1024,1024]{2,1,0:T(8,128)(2,1)} %grads_hbm.1, bf16[1024,1024]{1,0:T(8,128)(2,1)} %attn_hbm.1, f32[4,5]{1,0:T(4,128)} %coefs.1), custom_call_target="tpu_custom_call" | custom-call | tf_op jit(solution)/shard_map/pallas_call | solution.py:317
  137.0 1.2 copy.8
  138.3 3.2 %copy.9 = f32[512,1024]{1,0:T(8,128)} copy(f32[512,1024]{1,0:T(8,128)} %get-tuple-element.5) | data formatting | bytes 4194304
where the time goes:
time: 142 us; the launch traced here: 141 us
  Pallas kernels  136 us (96%)
  local copies, waits for them, and re-layouts  4.4 us (3%)
    pallas_call x1, Pallas kernels, local(): pl.pallas_call(functools.partial(kernel, dp_size, tensor_size), out_shape...  136 us
    unnamed x2, local copies, waits for them, and re-layouts  4.4 us

commit v1 on v0

v1 whole, which is shorter than its diff:
```python
import functools

import jax
import jax.numpy as jnp
from jax import lax
from jax.experimental import pallas as pl
from jax.experimental.pallas import tpu as pltpu
from jax.sharding import PartitionSpec as P

LANES = 128
LAG = 3
SKEW = 2


def kernel(
    dp_size, tensor_size, outs_hbm, grads_hbm, attn_hbm, coefs, coef_out, proj_out,
    outs, grads, attn, gathered, g_send, own, z_send, z_left, z_right, sums_ref, coef_a, coef_b, coef_c,
    load_sem, attn_sem, gy_sem, p_sem, x_sem, g_recv, a_sem, a_recv,
    z_send_sem, zl_sem, zr_sem, ca_send, ca_recv, cb_send, cb_recv,
):
    depth, tokens, features = grads.shape
    rows, cols = proj_out.shape
    strips = cols // LANES
    chunks = rows // LANES
    early = max(chunks // 2, 1)
    ys = dp_size // tensor_size
    zs = tensor_size
    xs = tensor_size // 2
    dp, tensor = lax.axis_index("dp"), lax.axis_index("tensor")
    z, y = dp // ys, dp % ys
    x, core = tensor // 2, tensor % 2
    partner = x * 2 + 1 - core
    beside = jnp.where(z == 0, 1, jnp.where(z == zs - 1, zs - 2, -1))
    two = min(2, strips)
    mesh_id = pl.DeviceIdType.MESH

    loads = []
    for i in (depth - 2, depth - 1):
        loads.append(pltpu.make_async_copy(grads_hbm.at[i], grads.at[i], load_sem.at[i]))
    for i in range(depth - 2):
        loads.append(pltpu.make_async_copy(grads_hbm.at[i], grads.at[i], load_sem.at[i]))
    for j in range(depth + 1):
        loads.append(pltpu.make_async_copy(outs_hbm.at[j], outs.at[j], load_sem.at[depth + j]))
    mine = pl.ds(pl.multiple_of(y * tokens, tokens), tokens)
    attn_loads = [
        pltpu.make_async_copy(
            attn_hbm.at[:, pl.ds(k * LANES, LANES)], attn.at[k, mine, :], attn_sem.at[k]
        )
        for k in range(strips)
    ]
    loads[0].start()
    loads[1].start()
    for load in attn_loads:
        load.start()
    for load in loads[2:]:
        load.start()

    barrier = pltpu.get_barrier_semaphore()

    def greet(**device):
        pl.semaphore_signal(barrier, inc=1, device_id=device, device_id_type=mesh_id)

    greet(tensor=partner)
    for i in range(1, ys):
        greet(dp=z * ys + (y + i) % ys)
    for n in range(1, xs):
        greet(tensor=(x + n) % xs * 2 + core)

    @pl.when(z > 0)
    def _():
        greet(dp=dp - ys)

    @pl.when(z < zs - 1)
    def _():
        greet(dp=dp + ys)

    def meet():
        ends = jnp.where(z == 0, 1, 0) + jnp.where(z == zs - 1, 1, 0)
        pl.semaphore_wait(barrier, 1 + (ys - 1) + (xs - 1) + 2 - ends)

    def lane_rows(c, count=1):
        return pl.ds(c * LANES, LANES * count)

    def piece(slot, part, c):
        return gathered.at[slot, part, lane_rows(c), :]

    def y_copy(i, c):
        return pltpu.make_async_remote_copy(
            src_ref=g_send.at[i - 1, lane_rows(c), :], dst_ref=piece(tensor, y, c),
            send_sem=gy_sem.at[i - 1, c], recv_sem=g_recv.at[tensor, y, c],
            device_id={"dp": z * ys + (y + i) % ys}, device_id_type=mesh_id,
        )

    def partner_copy(slot, part, c):
        return pltpu.make_async_remote_copy(
            src_ref=piece(slot, part, c), dst_ref=piece(slot, part, c),
            send_sem=p_sem.at[slot // 2, part, c], recv_sem=g_recv.at[slot, part, c],
            device_id={"tensor": partner}, device_id_type=mesh_id,
        )

    def x_copy(n, part, c):
        return pltpu.make_async_remote_copy(
            src_ref=piece(tensor, part, c), dst_ref=piece(tensor, part, c),
            send_sem=x_sem.at[n - 1, part, c], recv_sem=g_recv.at[tensor, part, c],
            device_id={"tensor": (x + n) % xs * 2 + core}, device_id_type=mesh_id,
        )

    def arrive(slot, part, c):
        partner_copy(slot, part, c).wait_recv()

    def attn_copy(i, k):
        return pltpu.make_async_remote_copy(
            src_ref=attn.at[k, mine, :], dst_ref=attn.at[k, mine, :],
            send_sem=a_sem.at[i - 1, k], recv_sem=a_recv.at[y, k],
            device_id={"dp": z * ys + (y + i) % ys}, device_id_type=mesh_id,
        )

    def attn_arrive(k):
        for i in range(1, ys):
            part = (y + i) % ys
            there = pl.ds(pl.multiple_of(part * tokens, tokens), tokens)
            pltpu.make_async_remote_copy(
                src_ref=attn.at[k, there, :], dst_ref=attn.at[k, there, :],
                send_sem=a_sem.at[i - 1, k], recv_sem=a_recv.at[part, k],
                device_id={"dp": z * ys + part}, device_id_type=mesh_id,
            ).wait_recv()

    def make(part, c, into):
        first, second = coefs[depth - 2, depth - 1], coefs[depth - 1, depth - 1]

        @pl.loop(0, tokens // LANES)
        def _(step):
            at = pl.ds(pl.multiple_of(step * LANES, LANES), LANES)
            wide = pl.ds(pl.multiple_of(part * rows + c * LANES, LANES), LANES)
            value = first * grads[depth - 2, at, wide].astype(jnp.float32)
            value += second * grads[depth - 1, at, wide].astype(jnp.float32)
            into[lane_rows(c), at] = value.T.astype(jnp.bfloat16)

    def make_sent(c):
        for i in range(1, ys):
            make((y + i) % ys, c, g_send.at[i - 1])

    def make_own(c):
        make(y, c, gathered.at[tensor, y])
        partner_copy(tensor, y, c).start()

    def send_y(c):
        for i in range(1, ys):
            y_copy(i, c).start()

    def send_x(part, c):
        for n in range(1, xs):
            x_copy(n, part, c).start()

    def send_attn():
        for k in range(strips):
            for i in range(1, ys):
                attn_copy(i, k).start()

    def relay_y(c):
        for i in range(1, ys):
            part = (y + i) % ys
            arrive(tensor, part, c)
            partner_copy(tensor, part, c).start()
            send_x(part, c)

    others = [((x + n) % xs) * 2 for n in range(1, xs)]

    def relay_x(part, c, when):
        for other in others:
            @pl.when(when(other + core))
            def _():
                arrive(other + core, part, c)
                partner_copy(other + core, part, c).start()

    messages = [(0, early, k, k + 1) for k in range(strips)]
    halves = [(0, strips // 2), (strips // 2, strips)] if strips > 1 else [(0, strips)]
    rest = chunks - early
    late = [(c, 1) + half for c in range(early, chunks) for half in halves]
    soon = [(early, rest, 0, two)] + [(early, rest, k, k + 1) for k in range(two, strips)] if rest else []
    late_ids = range(strips, strips + len(late))
    soon_ids = range(strips + len(late), strips + len(late) + len(soon))
    messages = messages + late + soon

    def window(m):
        c, count, k_first, k_end = messages[m]
        return pl.ds(k_first, k_end - k_first), pl.ds(c * LANES, LANES * count)

    def right_copy(slot, m):
        ks, at = window(m)
        return pltpu.make_async_remote_copy(
            src_ref=z_send.at[slot, ks, at, :], dst_ref=z_left.at[slot, ks, at, :],
            send_sem=z_send_sem.at[slot, m], recv_sem=zl_sem.at[slot, m],
            device_id={"dp": dp + ys}, device_id_type=mesh_id,
        )

    def left_copy(slot, m):
        ks, at = window(m)
        return pltpu.make_async_remote_copy(
            src_ref=z_send.at[slot, ks, at, :], dst_ref=z_right.at[slot, ks, at, :],
            send_sem=z_send_sem.at[slot, m], recv_sem=zr_sem.at[slot, m],
            device_id={"dp": dp - ys}, device_id_type=mesh_id,
        )

    def product(slot, k, c, count, width=1):
        at = pl.ds(c * LANES, LANES * count)
        left = jnp.concatenate([gathered[slot, part, at, :] for part in range(ys)], axis=1)
        right = jnp.concatenate([attn[k + n] for n in range(width)], axis=1)
        value = jnp.dot(left, right, preferred_element_type=jnp.float32)
        return [value[:, n * LANES : (n + 1) * LANES] for n in range(width)]

    def compute(slot, m):
        c, count, k_first, k_end = messages[m]
        at = pl.ds(c * LANES, LANES * count)
        rightmost, leftmost = (slot > z) & (z == 0), (slot < z) & (z == zs - 1)

        width = 2 - (k_end - k_first) % 2

        @pl.loop(k_first, k_end, step=width)
        def _(k):
            values = product(slot, k, c, count, width)

            @pl.when(rightmost | leftmost)
            def _():
                for n, value in enumerate(values):
                    z_send[slot, k + n, at, :] = value.astype(jnp.bfloat16)

            @pl.when(jnp.logical_not(rightmost | leftmost))
            def _():
                for n, value in enumerate(values):
                    own[slot, k + n, at, :] = value

        @pl.when(rightmost)
        def _():
            right_copy(slot, m).start()

        @pl.when(leftmost)
        def _():
            left_copy(slot, m).start()

    def pass_on(slot, m, hop):
        c, count, k_first, k_end = messages[m]
        at = pl.ds(c * LANES, LANES * count)

        @pl.when((slot > z) & (z == hop))
        def _():
            right_copy(slot, m).wait_recv()
            for k in range(k_first, k_end):
                value = own[slot, k, at, :] + z_left[slot, k, at, :].astype(jnp.float32)
                z_send[slot, k, at, :] = value.astype(jnp.bfloat16)
            right_copy(slot, m).start()

        @pl.when((slot < z) & (z == zs - 1 - hop))
        def _():
            left_copy(slot, m).wait_recv()
            for k in range(k_first, k_end):
                value = own[slot, k, at, :] + z_right[slot, k, at, :].astype(jnp.float32)
                z_send[slot, k, at, :] = value.astype(jnp.bfloat16)
            left_copy(slot, m).start()

    pairs = [(i, j) for i in range(depth) for j in range(min(i + 2, depth + 1))]
    quarters = 4

    def coef_partial(quarter):
        size = tokens // 16 // quarters

        def step(r, sums):
            at = pl.ds(pl.multiple_of(r * 16, 16), 16)
            sums = list(sums)
            for col in range(features // LANES):
                lanes = slice(col * LANES, (col + 1) * LANES)
                g = [grads[i, at, lanes].astype(jnp.float32) for i in range(depth)]
                o = [outs[j, at, lanes].astype(jnp.float32) for j in range(depth + 1)]
                for n, (i, j) in enumerate(pairs):
                    value = g[i] * o[j]
                    sums[n] += value[:8] + value[8:]
            return tuple(sums)

        zero = jnp.zeros((8, LANES), jnp.float32)
        first = tuple(zero if quarter == 0 else sums_ref[n] for n in range(len(pairs)))
        sums = lax.fori_loop(quarter * size, (quarter + 1) * size, step, first)
        for n in range(len(pairs)):
            sums_ref[n] = sums[n]

    def coef_tile():
        row = lax.broadcasted_iota(jnp.int32, (8, LANES), 0)
        col = lax.broadcasted_iota(jnp.int32, (8, LANES), 1)
        tile = jnp.zeros((8, LANES), jnp.float32)
        for n, (i, j) in enumerate(pairs):
            value = jnp.sum(sums_ref[n], axis=(0, 1), keepdims=True)
            tile = jnp.where((row == i) & (col == j), value, tile)
        return tile

    def coef_hop(stage, target):
        return pltpu.make_async_remote_copy(
            src_ref=coef_a.at[stage], dst_ref=coef_b.at[stage],
            send_sem=ca_send.at[stage], recv_sem=ca_recv.at[stage],
            device_id=target, device_id_type=mesh_id,
        )

    def coef_step(step):
        if step < zs:
            @pl.when(z == step)
            def _():
                coef_a[0] = coef_tile()
                if step > 0:
                    coef_hop(0, {"dp": dp + ys}).wait_recv()
                    coef_a[0] += coef_b[0]
                if step < zs - 1:
                    coef_hop(0, {"dp": dp + ys}).start()
                else:
                    coef_a[1] = coef_a[0]
                    coef_hop(1, {"dp": dp - ys}).start()
        else:
            plane = 2 * zs - 2 - step

            @pl.when(z == plane)
            def _():
                coef_hop(1, {"dp": dp - ys}).wait_recv()
                coef_a[1] = coef_b[1]
                if plane > 0:
                    coef_hop(1, {"dp": dp - ys}).start()

    def coef_partner(start):
        if start:
            coef_hop(2, {"tensor": partner}).start()
        else:
            coef_hop(2, {"tensor": partner}).wait_recv()

    def coef_x(n, at):
        return pltpu.make_async_remote_copy(
            src_ref=coef_c.at[at], dst_ref=coef_c.at[at],
            send_sem=cb_send.at[n], recv_sem=cb_recv.at[at],
            device_id={"tensor": (x + n) % xs * 2 + core}, device_id_type=mesh_id,
        )

    def coef_y(i, at):
        return pltpu.make_async_remote_copy(
            src_ref=coef_c.at[xs + at], dst_ref=coef_c.at[xs + at],
            send_sem=cb_send.at[xs + i], recv_sem=cb_recv.at[xs + at],
            device_id={"dp": z * ys + (y + i) % ys}, device_id_type=mesh_id,
        )

    last = tensor == z
    first = tensor == beside
    plain = jnp.logical_not(last | first)
    sooner = jnp.logical_not(last)
    parts = [y] + [(y + i) % ys for i in range(1, ys)]

    def away(slot):
        return slot != z

    def away_first(slot):
        return (slot != z) & first

    def away_plain(slot):
        return (slot != z) & jnp.logical_not(first)

    def home(slot):
        return slot == z

    def never(slot):
        return slot < 0

    def near(slot):
        return (slot != z) & (slot // 2 == x)

    def far(slot):
        return (slot != z) & (slot // 2 != x)

    def is_first(slot):
        return slot == beside

    def is_plain(slot):
        return (slot != z) & (slot != beside)

    def near_plain(slot):
        return near(slot) & (slot != beside)

    def far_plain(slot):
        return far(slot) & (slot != beside)

    def near_first(slot):
        return (slot == beside) & (slot // 2 == x)

    def far_first(slot):
        return (slot == beside) & (slot // 2 != x)

    def slot_at(i):
        outer = jnp.where(i % 2 == 0, zs - 1 - i // 2, i // 2)
        return jnp.where(z < zs // 2, outer, zs - 1 - outer)

    queue, clock = [], [0]

    def tick():
        for hop in range(1, zs - 1):
            index = clock[0] - LAG - (hop - 1) * SKEW
            if 0 <= index < len(queue):
                follow(*queue[index], hop)
        clock[0] += 1

    def follow(m, passed, hop):
        @pl.loop(0, zs)
        def _(i):
            slot = slot_at(i)

            @pl.when(passed(slot))
            def _():
                pass_on(slot, m, hop)

    def run(m, when, passed):
        @pl.loop(0, zs)
        def _(i):
            slot = slot_at(i)

            @pl.when(when(slot))
            def _():
                compute(slot, m)

        if passed is not never:
            queue.append((m, passed))
            tick()

    def gather_partner(slot, c_first, c_end, when):
        @pl.when(when(slot))
        def _():
            for c in range(c_first, c_end):
                for part in parts:
                    arrive(slot, part, c)

    steps = list(range(2 * zs - 1))
    share = -(-len(steps) // 7)

    def coef_steps():
        for step in steps[:share]:
            coef_step(step)
        del steps[:share]

    loads[0].wait()
    loads[1].wait()
    make_sent(0)
    meet()

    @pl.when(sooner)
    def _():
        send_y(0)

    make_own(0)

    @pl.when(sooner)
    def _():
        send_x(y, 0)

    for c in range(1, early):
        make_sent(c)

        @pl.when(sooner)
        def _():
            send_y(c)

    @pl.when(first)
    def _():
        for c in range(early, chunks):
            make_sent(c)
            send_y(c)

    for load in attn_loads:
        load.wait()
    send_attn()
    for c in range(1, early):
        make_own(c)
    for load in loads[2:]:
        load.wait()

    coef_partial(0)
    for c in range(early):
        @pl.when(sooner)
        def _():
            relay_y(c)
            if c + 1 < early:
                send_x(y, c + 1)

        if c == 0:
            relay_x(y, 0, away)
        coef_partial(1 + c if early > 1 else 1)
    for quarter in range(1 + max(early, 1), quarters):
        coef_partial(quarter)
    coef_steps()
    for part in parts[1:]:
        relay_x(part, 0, away)

    @pl.when(first)
    def _():
        for c in range(early, chunks):
            make_own(c)
            send_x(y, c)
            relay_y(c)

    for c in range(1, early):
        relay_x(y, c, away_first)

    attn_arrive(0)
    gather_partner(partner, 0, early, away)
    run(0, near, near)
    coef_steps()
    for c in range(1, early):
        relay_x(y, c, away_plain)
        for part in parts[1:]:
            relay_x(part, c, away_first)
    coef_steps()
    if two > 1:
        attn_arrive(1)
        run(1, near, near)
    coef_steps()
    for c in range(1, early):
        for part in parts[1:]:
            relay_x(part, c, away_plain)
    soon_left = list(soon_ids)
    if rest:
        gather_partner(partner, early, chunks, is_first)
        run(soon_left[0], near_first, never)
    for other in others:
        gather_partner(other + 1 - core, 0, early, away)
    for k in range(two):
        run(k, far, far)
    if rest:
        for c in range(early, chunks):
            for part in parts:
                relay_x(part, c, is_first)
        for other in others:
            gather_partner(other + 1 - core, early, chunks, is_first)
        run(soon_left.pop(0), far_first, never)

        @pl.when(plain | last)
        def _():
            for c in range(early, chunks):
                make_sent(c)

        @pl.when(plain)
        def _():
            for c in range(early, chunks):
                send_y(c)

        @pl.when(plain | last)
        def _():
            for c in range(early, chunks):
                make_own(c)

        @pl.when(plain)
        def _():
            for c in range(early, chunks):
                send_x(y, c)

    @pl.when(last)
    def _():
        for c in range(chunks):
            send_y(c)

    for k in range(two, strips):
        attn_arrive(k)
        run(k, away, away)
        if soon_left:
            run(soon_left.pop(0), is_first, never)
        if k % 2:
            coef_steps()
        if k == strips // 2:
            @pl.when(last)
            def _():
                for c in range(chunks):
                    send_x(y, c)
    while steps:
        coef_steps()
    coef_a[2] = coef_a[1]
    coef_partner(True)

    for c in range(early, chunks):
        relay_x(y, c, is_plain)
    for c in range(chunks):
        relay_x(y, c, home)
    behind = list(range(chunks))
    for c in range(early, chunks):
        @pl.when(plain)
        def _():
            relay_y(c)

        now, behind = behind[: -(-chunks // max(rest, 1))], behind[-(-chunks // max(rest, 1)):]

        @pl.when(last)
        def _():
            for d in now:
                relay_y(d)

        gather_partner(partner, c, c + 1, is_plain)
        for h in range(len(halves)):
            run(late_ids[(c - early) * len(halves) + h], near_plain, near)

    @pl.when(last)
    def _():
        for d in behind:
            relay_y(d)

    for c in range(early, chunks):
        for part in parts[1:]:
            relay_x(part, c, is_plain)
        if c == early:
            coef_partner(False)
            coef_c[x] = coef_a[2] + coef_b[2]
            for n in range(1, xs):
                coef_x(n, x).start()
        for other in others:
            gather_partner(other + 1 - core, c, c + 1, is_plain)
        for h in range(len(halves)):
            run(late_ids[(c - early) * len(halves) + h], far_plain, far)
    if not rest:
        coef_partner(False)
        coef_c[x] = coef_a[2] + coef_b[2]
        for n in range(1, xs):
            coef_x(n, x).start()
    for n in range(1, xs):
        coef_x(n, (x + n) % xs).wait_recv()
    total = coef_c[0]
    for n in range(1, xs):
        total += coef_c[n]
    coef_c[xs + y] = total
    for i in range(1, ys):
        coef_y(i, y).start()

    for c in range(chunks):
        for part in parts[1:]:
            relay_x(part, c, home)
    for _ in range(LAG + (zs - 3) * SKEW):
        tick()

    @pl.when(z % 2 != core)
    def _():
        for c in range(chunks):
            for part in parts:
                arrive(z, part, c)

    width = 2 - strips % 2

    @pl.loop(0, strips, step=width)
    def _(k):
        for n, value in enumerate(product(z, k, 0, chunks, width)):
            own[z, k + n] = value

    for i in range(1, ys):
        coef_y(i, (y + i) % ys).wait_recv()
    total = coef_c[xs]
    for i in range(1, ys):
        total += coef_c[xs + i]
    coef_out[...] = total[: coef_out.shape[0], : coef_out.shape[1]]

    def from_left(ids):
        for m in ids:
            right_copy(z, m).wait_recv()

    def from_right(ids):
        for m in ids:
            left_copy(z, m).wait_recv()

    @pl.when(z > 0)
    def _():
        from_left(range(strips))

    @pl.when(z < zs - 1)
    def _():
        from_right(range(strips))

    if rest:
        @pl.when(z == 1)
        def _():
            from_left(soon_ids)

        @pl.when(z > 1)
        def _():
            from_left(late_ids)

        @pl.when(z == zs - 2)
        def _():
            from_right(soon_ids)

        @pl.when(z < zs - 2)
        def _():
            from_right(late_ids)

    for k in range(strips):
        lanes = slice(k * LANES, (k + 1) * LANES)
        proj_out[:, lanes] = own[z, k]

        @pl.when(z > 0)
        def _():
            proj_out[:, lanes] += z_left[z, k].astype(jnp.float32)

        @pl.when(z < zs - 1)
        def _():
            proj_out[:, lanes] += z_right[z, k].astype(jnp.float32)

    @pl.loop(0, zs)
    def _(slot):
        @pl.when(slot != z)
        def _():
            for m in range(strips):
                right_copy(slot, m).wait_send()

        @pl.when(slot == beside)
        def _():
            for m in soon_ids:
                right_copy(slot, m).wait_send()

        @pl.when(is_plain(slot))
        def _():
            for m in late_ids:
                right_copy(slot, m).wait_send()

    for c in range(chunks):
        for i in range(1, ys):
            y_copy(i, c).wait_send()
        for part in range(ys):
            for n in range(xs):
                partner_copy(n * 2 + core, part, c).wait_send()
            for n in range(1, xs):
                x_copy(n, part, c).wait_send()
    for k in range(strips):
        for i in range(1, ys):
            attn_copy(i, k).wait_send()

    @pl.when(z < zs - 1)
    def _():
        coef_hop(0, {"dp": dp + ys}).wait_send()

    @pl.when(z > 0)
    def _():
        coef_hop(1, {"dp": dp - ys}).wait_send()

    coef_hop(2, {"tensor": partner}).wait_send()
    for n in range(1, xs):
        coef_x(n, x).wait_send()
    for i in range(1, ys):
        coef_y(i, y).wait_send()


def local(dp_size, tensor_size, layer_outs, avg_grads, attn_mixed, dwa_coefs):
    depth, tokens, features = avg_grads.shape
    rows = features * tensor_size // dp_size
    cols = attn_mixed.shape[1]
    ys, zs, xs = dp_size // tensor_size, tensor_size, tensor_size // 2
    strips, chunks = cols // LANES, rows // LANES
    bf16, f32 = jnp.bfloat16, jnp.float32
    dma = pltpu.SemaphoreType.DMA
    any_space = pl.BlockSpec(memory_space=pl.ANY)
    vmem = pl.BlockSpec(memory_space=pltpu.VMEM)
    return pl.pallas_call(
        functools.partial(kernel, dp_size, tensor_size),
        out_shape=(
            jax.ShapeDtypeStruct(dwa_coefs.shape, f32),
            jax.ShapeDtypeStruct((rows, cols), f32),
        ),
        in_specs=[any_space, any_space, any_space, pl.BlockSpec(memory_space=pltpu.SMEM)],
        out_specs=(vmem, vmem),
        scratch_shapes=[
            pltpu.VMEM(layer_outs.shape, bf16),
            pltpu.VMEM(avg_grads.shape, bf16),
            pltpu.VMEM((strips, ys * tokens, LANES), bf16),
            pltpu.VMEM((zs, ys, rows, tokens), bf16),
            pltpu.VMEM((ys - 1, rows, tokens), bf16),
            pltpu.VMEM((zs, strips, rows, LANES), f32),
            pltpu.VMEM((zs, strips, rows, LANES), bf16),
            pltpu.VMEM((zs, strips, rows, LANES), bf16),
            pltpu.VMEM((zs, strips, rows, LANES), bf16),
            pltpu.VMEM((depth * (depth + 1), 8, LANES), f32),
            pltpu.VMEM((3, 8, LANES), f32),
            pltpu.VMEM((3, 8, LANES), f32),
            pltpu.VMEM((xs + ys, 8, LANES), f32),
            dma((2 * depth + 1,)),
            dma((strips,)),
            dma((ys - 1, chunks)),
            dma((xs, ys, chunks)),
            dma((max(xs - 1, 1), ys, chunks)),
            dma((tensor_size, ys, chunks)),
            dma((ys - 1, strips)),
            dma((ys, strips)),
            dma((zs, 2 * strips + 2 * chunks)),
            dma((zs, 2 * strips + 2 * chunks)),
            dma((zs, 2 * strips + 2 * chunks)),
            dma((3,)),
            dma((3,)),
            dma((xs + ys,)),
            dma((xs + ys,)),
        ],
        compiler_params=pltpu.CompilerParams(
            collective_id=0, has_side_effects=True, vmem_limit_bytes=67000000
        ),
    )(layer_outs, avg_grads, attn_mixed, dwa_coefs)


def solution(mesh):
    sizes = (mesh.shape["dp"], mesh.shape["tensor"])
    in_specs = (P(None, "dp", "tensor"), P(None, "dp", "tensor"), P("dp", "tensor"), P())
    out_specs = (P(), P("dp", "tensor"))
    return jax.shard_map(
        functools.partial(local, *sizes), mesh=mesh, in_specs=in_specs, out_specs=out_specs, check_vma=False
    )
```

time: 142 us -> 129 us (0.908)
  the two profiles are of different devices: /device:TPU:17 before, /device:TPU:2 now
where the time goes in v1:
time: 129 us
  Pallas kernels  124 us (96%)
  local copies, waits for them, and re-layouts  4.4 us (3%)
    pallas_call x1, Pallas kernels, local(): pl.pallas_call(functools.partial(kernel, dp_size, tensor_size), out_shape...  124 us
    unnamed x2, local copies, waits for them, and re-layouts  4.4 us

profile of v1, /device:TPU:2, one launch (start us, length us, event | category | flops | bytes accessed | tf_op | source)
XLA Modules:
  0.0 129.2 jit_solution(7501183831866686794)
XLA Ops:
  0.6 124.1 %shard_map.59 = (f32[4,5]{1,0:T(4,128)}, f32[512,1024]{1,0:T(8,128)}) custom-call(bf16[5,1024,1024]{2,1,0:T(8,128)(2,1)} %outs_hbm.1, bf16[4,1024,1024]{2,1,0:T(8,128)(2,1)} %grads_hbm.1, bf16[1024,1024]{1,0:T(8,128)(2,1)} %attn_hbm.1, f32[4,5]{1,0:T(4,128)} %coefs.1), custom_call_target="tpu_custom_call" | custom-call | tf_op jit(solution)/shard_map/pallas_call | solution.py:753
  124.8 1.2 copy.8
  126.0 3.2 %copy.9 = f32[512,1024]{1,0:T(8,128)} copy(f32[512,1024]{1,0:T(8,128)} %get-tuple-element.5) | data formatting | bytes 4194304

commit v2 on v1

--- a/solution.py
+++ b/solution.py
@@ -8,18 +8,18 @@
 from jax.sharding import PartitionSpec as P
 
 LANES = 128
-LAG = 3
+LAG = 1
 SKEW = 2
 
 
 def kernel(
     dp_size, tensor_size, outs_hbm, grads_hbm, attn_hbm, coefs, coef_out, proj_out,
-    outs, grads, attn, gathered, g_send, own, z_send, z_left, z_right, sums_ref, coef_a, coef_b, coef_c,
+    outs, grads, attn, gathered, g_send, own, z_send, z_left, z_right, sums_ref, coef_a, coef_b, coef_c, result,
     load_sem, attn_sem, gy_sem, p_sem, x_sem, g_recv, a_sem, a_recv,
-    z_send_sem, zl_sem, zr_sem, ca_send, ca_recv, cb_send, cb_recv,
+    z_send_sem, z_sem, ca_send, ca_recv, cb_send, cb_recv,
 ):
     depth, tokens, features = grads.shape
-    rows, cols = proj_out.shape
+    rows, cols = result.shape
     strips = cols // LANES
     chunks = rows // LANES
     early = max(chunks // 2, 1)
@@ -44,7 +44,7 @@
     mine = pl.ds(pl.multiple_of(y * tokens, tokens), tokens)
     attn_loads = [
         pltpu.make_async_copy(
-            attn_hbm.at[:, pl.ds(k * LANES, LANES)], attn.at[k, mine, :], attn_sem.at[k]
+            attn_hbm.at[:, pl.ds(k * LANES, LANES)], attn.at[k, mine, :], attn_sem
         )
         for k in range(strips)
     ]
@@ -87,21 +87,21 @@
     def y_copy(i, c):
         return pltpu.make_async_remote_copy(
             src_ref=g_send.at[i - 1, lane_rows(c), :], dst_ref=piece(tensor, y, c),
-            send_sem=gy_sem.at[i - 1, c], recv_sem=g_recv.at[tensor, y, c],
+            send_sem=gy_sem.at[i - 1], recv_sem=g_recv.at[tensor, y, c],
             device_id={"dp": z * ys + (y + i) % ys}, device_id_type=mesh_id,
         )
 
     def partner_copy(slot, part, c):
         return pltpu.make_async_remote_copy(
             src_ref=piece(slot, part, c), dst_ref=piece(slot, part, c),
-            send_sem=p_sem.at[slot // 2, part, c], recv_sem=g_recv.at[slot, part, c],
+            send_sem=p_sem.at[slot // 2], recv_sem=g_recv.at[slot, part, c],
             device_id={"tensor": partner}, device_id_type=mesh_id,
         )
 
     def x_copy(n, part, c):
         return pltpu.make_async_remote_copy(
             src_ref=piece(tensor, part, c), dst_ref=piece(tensor, part, c),
-            send_sem=x_sem.at[n - 1, part, c], recv_sem=g_recv.at[tensor, part, c],
+            send_sem=x_sem.at[n - 1], recv_sem=g_recv.at[tensor, part, c],
             device_id={"tensor": (x + n) % xs * 2 + core}, device_id_type=mesh_id,
         )
 
@@ -111,7 +111,7 @@
     def attn_copy(i, k):
         return pltpu.make_async_remote_copy(
             src_ref=attn.at[k, mine, :], dst_ref=attn.at[k, mine, :],
-            send_sem=a_sem.at[i - 1, k], recv_sem=a_recv.at[y, k],
+            send_sem=a_sem.at[i - 1], recv_sem=a_recv.at[ys - i - 1, k],
             device_id={"dp": z * ys + (y + i) % ys}, device_id_type=mesh_id,
         )
 
@@ -121,7 +121,7 @@
             there = pl.ds(pl.multiple_of(part * tokens, tokens), tokens)
             pltpu.make_async_remote_copy(
                 src_ref=attn.at[k, there, :], dst_ref=attn.at[k, there, :],
-                send_sem=a_sem.at[i - 1, k], recv_sem=a_recv.at[part, k],
+                send_sem=a_sem.at[i - 1], recv_sem=a_recv.at[i - 1, k],
                 device_id={"dp": z * ys + part}, device_id_type=mesh_id,
             ).wait_recv()
 
@@ -186,21 +186,34 @@
         c, count, k_first, k_end = messages[m]
         return pl.ds(k_first, k_end - k_first), pl.ds(c * LANES, LANES * count)
 
-    def right_copy(slot, m):
+    passing = strips + len(late)
+
+    def arrival(slot, m):
+        return slot * passing + m
+
+    def right_copy(slot, m, sem):
         ks, at = window(m)
         return pltpu.make_async_remote_copy(
             src_ref=z_send.at[slot, ks, at, :], dst_ref=z_left.at[slot, ks, at, :],
-            send_sem=z_send_sem.at[slot, m], recv_sem=zl_sem.at[slot, m],
+            send_sem=z_send_sem.at[slot], recv_sem=z_sem.at[sem],
             device_id={"dp": dp + ys}, device_id_type=mesh_id,
         )
 
-    def left_copy(slot, m):
+    def left_copy(slot, m, sem):
         ks, at = window(m)
         return pltpu.make_async_remote_copy(
             src_ref=z_send.at[slot, ks, at, :], dst_ref=z_right.at[slot, ks, at, :],
-            send_sem=z_send_sem.at[slot, m], recv_sem=zr_sem.at[slot, m],
+            send_sem=z_send_sem.at[slot], recv_sem=z_sem.at[sem],
             device_id={"dp": dp - ys}, device_id_type=mesh_id,
         )
+
+    def send_right(slot, m):
+        sem = zs * passing if m in soon_ids else jnp.where(slot == z + 1, zs * passing, arrival(slot, m))
+        right_copy(slot, m, sem).start()
+
+    def send_left(slot, m):
+        sem = zs * passing + 1 if m in soon_ids else jnp.where(slot == z - 1, zs * passing + 1, arrival(slot, m))
+        left_copy(slot, m, sem).start()
 
     def product(slot, k, c, count, width=1):
         at = pl.ds(c * LANES, LANES * count)
@@ -232,11 +245,11 @@
 
         @pl.when(rightmost)
         def _():
-            right_copy(slot, m).start()
+            send_right(slot, m)
 
         @pl.when(leftmost)
         def _():
-            left_copy(slot, m).start()
+            send_left(slot, m)
 
     def pass_on(slot, m, hop):
         c, count, k_first, k_end = messages[m]
@@ -244,19 +257,19 @@
 
         @pl.when((slot > z) & (z == hop))
         def _():
-            right_copy(slot, m).wait_recv()
+            right_copy(slot, m, arrival(slot, m)).wait_recv()
             for k in range(k_first, k_end):
                 value = own[slot, k, at, :] + z_left[slot, k, at, :].astype(jnp.float32)
                 z_send[slot, k, at, :] = value.astype(jnp.bfloat16)
-            right_copy(slot, m).start()
+            send_right(slot, m)
 
         @pl.when((slot < z) & (z == zs - 1 - hop))
         def _():
-            left_copy(slot, m).wait_recv()
+            left_copy(slot, m, arrival(slot, m)).wait_recv()
             for k in range(k_first, k_end):
                 value = own[slot, k, at, :] + z_right[slot, k, at, :].astype(jnp.float32)
                 z_send[slot, k, at, :] = value.astype(jnp.bfloat16)
-            left_copy(slot, m).start()
+            send_left(slot, m)
 
     pairs = [(i, j) for i in range(depth) for j in range(min(i + 2, depth + 1))]
     quarters = 4
@@ -390,36 +403,49 @@
         outer = jnp.where(i % 2 == 0, zs - 1 - i // 2, i // 2)
         return jnp.where(z < zs // 2, outer, zs - 1 - outer)
 
-    queue, clock = [], [0]
+    def late_of(c):
+        return late_ids[(c - early) * len(halves) : (c - early + 1) * len(halves)]
+
+    queue, done = [], {hop: 0 for hop in range(1, zs - 1)}
+
+    def advance(hop, limit):
+        while hop in done and done[hop] < min(limit, len(queue)):
+            follow(*queue[done[hop]], hop)
+            done[hop] += 1
 
     def tick():
-        for hop in range(1, zs - 1):
-            index = clock[0] - LAG - (hop - 1) * SKEW
-            if 0 <= index < len(queue):
-                follow(*queue[index], hop)
-        clock[0] += 1
-
-    def follow(m, passed, hop):
+        for hop in done:
+            advance(hop, len(queue) - LAG - (hop - 1) * SKEW)
+
+    def flush():
+        while any(place < len(queue) for place in done.values()):
+            for hop in done:
+                ahead = done.get(hop - 1, len(queue))
+                limit = ahead if ahead == len(queue) else ahead - 1
+                advance(hop, min(done[hop] + hop, limit))
+
+    def follow(ms, passed, hop):
         @pl.loop(0, zs)
         def _(i):
             slot = slot_at(i)
 
             @pl.when(passed(slot))
             def _():
-                pass_on(slot, m, hop)
-
-    def run(m, when, passed):
+                for m in ms:
+                    pass_on(slot, m, hop)
+
+    def run(ms, when, passed):
         @pl.loop(0, zs)
         def _(i):
             slot = slot_at(i)
 
             @pl.when(when(slot))
             def _():
-                compute(slot, m)
+                for m in ms:
+                    compute(slot, m)
 
         if passed is not never:
-            queue.append((m, passed))
-            tick()
+            queue.append((ms, passed))
 
     def gather_partner(slot, c_first, c_end, when):
         @pl.when(when(slot))
@@ -464,8 +490,7 @@
             make_sent(c)
             send_y(c)
 
-    for load in attn_loads:
-        load.wait()
+    pltpu.make_async_copy(attn.at[:, mine, :], attn.at[:, mine, :], attn_sem).wait()
     send_attn()
     for c in range(1, early):
         make_own(c)
@@ -501,7 +526,8 @@
 
     attn_arrive(0)
     gather_partner(partner, 0, early, away)
-    run(0, near, near)
+    run([0], near, near)
+    tick()
     coef_steps()
     for c in range(1, early):
         relay_x(y, c, away_plain)
@@ -510,7 +536,8 @@
     coef_steps()
     if two > 1:
         attn_arrive(1)
-        run(1, near, near)
+        run([1], near, near)
+        tick()
     coef_steps()
     for c in range(1, early):
         for part in parts[1:]:
@@ -518,18 +545,19 @@
     soon_left = list(soon_ids)
     if rest:
         gather_partner(partner, early, chunks, is_first)
-        run(soon_left[0], near_first, never)
+        run([soon_left[0]], near_first, never)
     for other in others:
         gather_partner(other + 1 - core, 0, early, away)
     for k in range(two):
-        run(k, far, far)
+        run([k], far, far)
+        tick()
     if rest:
         for c in range(early, chunks):
             for part in parts:
                 relay_x(part, c, is_first)
         for other in others:
             gather_partner(other + 1 - core, early, chunks, is_first)
-        run(soon_left.pop(0), far_first, never)
+        run([soon_left.pop(0)], far_first, never)
 
         @pl.when(plain | last)
         def _():
@@ -558,12 +586,13 @@
 
     for k in range(two, strips):
         attn_arrive(k)
-        run(k, away, away)
+        run([k], away, away)
+        tick()
         if soon_left:
-            run(soon_left.pop(0), is_first, never)
+            run([soon_left.pop(0)], is_first, never)
         if k % 2:
             coef_steps()
-        if k == strips // 2:
+        if k == two:
             @pl.when(last)
             def _():
                 for c in range(chunks):
@@ -578,6 +607,7 @@
     for c in range(chunks):
         relay_x(y, c, home)
     behind = list(range(chunks))
+    started = len(queue)
     for c in range(early, chunks):
         @pl.when(plain)
         def _():
@@ -591,13 +621,15 @@
                 relay_y(d)
 
         gather_partner(partner, c, c + 1, is_plain)
-        for h in range(len(halves)):
-            run(late_ids[(c - early) * len(halves) + h], near_plain, near)
+        run(late_of(c), near_plain, near)
+        advance(1, len(queue) - LAG)
 
     @pl.when(last)
     def _():
         for d in behind:
             relay_y(d)
+
+    advance(2, started)
 
     for c in range(early, chunks):
         for part in parts[1:]:
@@ -609,8 +641,9 @@
                 coef_x(n, x).start()
         for other in others:
             gather_partner(other + 1 - core, c, c + 1, is_plain)
-        for h in range(len(halves)):
-            run(late_ids[(c - early) * len(halves) + h], far_plain, far)
+        run(late_of(c), far_plain, far)
+        advance(1, len(queue) - LAG)
+        advance(2, started + c - early)
     if not rest:
         coef_partner(False)
         coef_c[x] = coef_a[2] + coef_b[2]
@@ -628,8 +661,7 @@
     for c in range(chunks):
         for part in parts[1:]:
             relay_x(part, c, home)
-    for _ in range(LAG + (zs - 3) * SKEW):
-        tick()
+    flush()
 
     @pl.when(z % 2 != core)
     def _():
@@ -649,81 +681,65 @@
     total = coef_c[xs]
     for i in range(1, ys):
         total += coef_c[xs + i]
-    coef_out[...] = total[: coef_out.shape[0], : coef_out.shape[1]]
-
-    def from_left(ids):
-        for m in ids:
-            right_copy(z, m).wait_recv()
-
-    def from_right(ids):
-        for m in ids:
-            left_copy(z, m).wait_recv()
+    coef_b[2] = total
+    coef_store = pltpu.make_async_copy(coef_b.at[2], coef_out, load_sem.at[0])
+    coef_store.start()
 
     @pl.when(z > 0)
     def _():
-        from_left(range(strips))
+        pltpu.make_async_remote_copy(
+            src_ref=z_left.at[z], dst_ref=z_left.at[z],
+            send_sem=z_send_sem.at[z], recv_sem=z_sem.at[zs * passing],
+            device_id={"dp": dp - ys}, device_id_type=mesh_id,
+        ).wait_recv()
 
     @pl.when(z < zs - 1)
     def _():
-        from_right(range(strips))
-
-    if rest:
-        @pl.when(z == 1)
-        def _():
-            from_left(soon_ids)
-
-        @pl.when(z > 1)
-        def _():
-            from_left(late_ids)
-
-        @pl.when(z == zs - 2)
-        def _():
-            from_right(soon_ids)
-
-        @pl.when(z < zs - 2)
-        def _():
-            from_right(late_ids)
-
-    for k in range(strips):
-        lanes = slice(k * LANES, (k + 1) * LANES)
-        proj_out[:, lanes] = own[z, k]
-
-        @pl.when(z > 0)
-        def _():
-            proj_out[:, lanes] += z_left[z, k].astype(jnp.float32)
-
-        @pl.when(z < zs - 1)
-        def _():
-            proj_out[:, lanes] += z_right[z, k].astype(jnp.float32)
+        pltpu.make_async_remote_copy(
+            src_ref=z_right.at[z], dst_ref=z_right.at[z],
+            send_sem=z_send_sem.at[z], recv_sem=z_sem.at[zs * passing + 1],
+            device_id={"dp": dp + ys}, device_id_type=mesh_id,
+        ).wait_recv()
+
+    for c in range(chunks):
+        at = lane_rows(c)
+        for k in range(strips):
+            lanes = slice(k * LANES, (k + 1) * LANES)
+            result[at, lanes] = own[z, k, at, :]
+
+            @pl.when(z > 0)
+            def _():
+                result[at, lanes] += z_left[z, k, at, :].astype(jnp.float32)
+
+            @pl.when(z < zs - 1)
+            def _():
+                result[at, lanes] += z_right[z, k, at, :].astype(jnp.float32)
+
+        pltpu.make_async_copy(result.at[at, :], proj_out.at[at, :], attn_sem).start()
 
     @pl.loop(0, zs)
     def _(slot):
         @pl.when(slot != z)
         def _():
-            for m in range(strips):
-                right_copy(slot, m).wait_send()
-
-        @pl.when(slot == beside)
-        def _():
-            for m in soon_ids:
-                right_copy(slot, m).wait_send()
-
-        @pl.when(is_plain(slot))
-        def _():
-            for m in late_ids:
-                right_copy(slot, m).wait_send()
-
-    for c in range(chunks):
-        for i in range(1, ys):
-            y_copy(i, c).wait_send()
-        for part in range(ys):
-            for n in range(xs):
-                partner_copy(n * 2 + core, part, c).wait_send()
-            for n in range(1, xs):
-                x_copy(n, part, c).wait_send()
-    for k in range(strips):
-        for i in range(1, ys):
-            attn_copy(i, k).wait_send()
+            pltpu.make_async_remote_copy(
+                src_ref=z_send.at[slot], dst_ref=z_left.at[slot],
+                send_sem=z_send_sem.at[slot], recv_sem=z_sem.at[0],
+                device_id={"dp": z * ys + (y + 1) % ys}, device_id_type=mesh_id,
+            ).wait_send()
+
+    def sent(ref, sem):
+        pltpu.make_async_remote_copy(
+            src_ref=ref, dst_ref=ref, send_sem=sem, recv_sem=z_sem.at[0],
+            device_id={"tensor": partner}, device_id_type=mesh_id,
+        ).wait_send()
+
+    for i in range(1, ys):
+        sent(g_send.at[i - 1], gy_sem.at[i - 1])
+        sent(attn.at[:, mine, :], a_sem.at[i - 1])
+    for n in range(xs):
+        sent(gathered.at[n * 2 + core], p_sem.at[n])
+    for n in range(1, xs):
+        sent(gathered.at[tensor], x_sem.at[n - 1])
 
     @pl.when(z < zs - 1)
     def _():
@@ -738,6 +754,13 @@
         coef_x(n, x).wait_send()
     for i in range(1, ys):
         coef_y(i, y).wait_send()
+    coef_store.wait()
+    pltpu.make_async_copy(result, proj_out, attn_sem).wait()
+
+
+def settle(coef, proj, coef_out, proj_out):
+    coef_out[...] = coef[: coef_out.shape[0], : coef_out.shape[1]]
+    proj_out[...] = proj[...]
 
 
 def local(dp_size, tensor_size, layer_outs, avg_grads, attn_mixed, dwa_coefs):
@@ -749,15 +772,14 @@
     bf16, f32 = jnp.bfloat16, jnp.float32
     dma = pltpu.SemaphoreType.DMA
     any_space = pl.BlockSpec(memory_space=pl.ANY)
-    vmem = pl.BlockSpec(memory_space=pltpu.VMEM)
-    return pl.pallas_call(
+    coef, proj = pl.pallas_call(
         functools.partial(kernel, dp_size, tensor_size),
         out_shape=(
-            jax.ShapeDtypeStruct(dwa_coefs.shape, f32),
+            jax.ShapeDtypeStruct((8, LANES), f32),
             jax.ShapeDtypeStruct((rows, cols), f32),
         ),
         in_specs=[any_space, any_space, any_space, pl.BlockSpec(memory_space=pltpu.SMEM)],
-        out_specs=(vmem, vmem),
+        out_specs=(any_space, any_space),
         scratch_shapes=[
             pltpu.VMEM(layer_outs.shape, bf16),
             pltpu.VMEM(avg_grads.shape, bf16),
@@ -772,17 +794,17 @@
             pltpu.VMEM((3, 8, LANES), f32),
             pltpu.VMEM((3, 8, LANES), f32),
             pltpu.VMEM((xs + ys, 8, LANES), f32),
+            pltpu.VMEM((rows, cols), f32),
             dma((2 * depth + 1,)),
-            dma((strips,)),
-            dma((ys - 1, chunks)),
-            dma((xs, ys, chunks)),
-            dma((max(xs - 1, 1), ys, chunks)),
+            dma,
+            dma((ys - 1,)),
+            dma((xs,)),
+            dma((max(xs - 1, 1),)),
             dma((tensor_size, ys, chunks)),
+            dma((ys - 1,)),
             dma((ys - 1, strips)),
-            dma((ys, strips)),
-            dma((zs, 2 * strips + 2 * chunks)),
-            dma((zs, 2 * strips + 2 * chunks)),
-            dma((zs, 2 * strips + 2 * chunks)),
+            dma((zs,)),
+            dma((zs * (strips + chunks) + 2,)),
             dma((3,)),
             dma((3,)),
             dma((xs + ys,)),
@@ -792,6 +814,23 @@
             collective_id=0, has_side_effects=True, vmem_limit_bytes=67000000
         ),
     )(layer_outs, avg_grads, attn_mixed, dwa_coefs)
+    half = rows // 2
+    return pl.pallas_call(
+        settle,
+        grid=(2,),
+        out_shape=(
+            jax.ShapeDtypeStruct(dwa_coefs.shape, f32),
+            jax.ShapeDtypeStruct((rows, cols), f32),
+        ),
+        in_specs=[
+            pl.BlockSpec((8, LANES), lambda i: (0, 0)),
+            pl.BlockSpec((half, cols), lambda i: (i, 0)),
+        ],
+        out_specs=(
+            pl.BlockSpec(dwa_coefs.shape, lambda i: (0, 0)),
+            pl.BlockSpec((half, cols), lambda i: (i, 0)),
+        ),
+    )(coef, proj)
 
 
 def solution(mesh):

time: 129 us -> 120 us (0.930)
  Pallas kernels: 124 us -> 119 us
  local copies, waits for them, and re-layouts: 4.4 us -> 0 us
    pallas_call x1, Pallas kernels: 124 us -> 116 us  [local(): pl.pallas_call(functools.partial(kernel, dp_size, tensor_size), out_shape...]
    unnamed x2 -> x0, local copies, waits for them, and re-layouts: 4.4 us -> none
    pallas_call x0 -> x1, Pallas kernels: none -> 2.63 us  [local(): pl.pallas_call(settle, grid=(2,), out_shape=(jax.ShapeDtypeStruct(dwa_coe...]
where the time goes in v2:
time: 120 us
  Pallas kernels  119 us (99%)
    pallas_call x1, Pallas kernels, local(): pl.pallas_call(functools.partial(kernel, dp_size, tensor_size), out_shape...  116 us
    pallas_call x1, Pallas kernels, local(): pl.pallas_call(settle, grid=(2,), out_shape=(jax.ShapeDtypeStruct(dwa_coe...  2.63 us

profile of v2, /device:TPU:2, one launch (start us, length us, event | category | flops | bytes accessed | tf_op | source)
XLA Modules:
  0.0 119.7 jit_solution(1290202979376277016)
XLA Ops:
  0.6 116.4 %shard_map.59 = (f32[8,128]{1,0:T(8,128)}, f32[512,1024]{1,0:T(8,128)}) custom-call(bf16[5,1024,1024]{2,1,0:T(8,128)(2,1)} %outs_hbm.1, bf16[4,1024,1024]{2,1,0:T(8,128)(2,1)} %grads_hbm.1, bf16[1024,1024]{1,0:T(8,128)(2,1)} %attn_hbm.1, f32[4,5]{1,0:T(4,128)} %coefs.1), custom_call_target="tpu_custom_call" | custom-call | tf_op jit(solution)/shard_map/pallas_call | solution.py:775
  117.1 2.6 %shard_map.60 = (f32[4,5]{1,0:T(4,128)}, f32[512,1024]{1,0:T(8,128)}) custom-call(f32[8,128]{1,0:T(8,128)} %get-tuple-element.4.coef, f32[512,1024]{1,0:T(8,128)} %get-tuple-element.5.proj), custom_call_target="tpu_custom_call" | custom-call | tf_op jit(solution)/shard_map/pallas_call | solution.py:818

commit v3 on v2

--- a/solution.py
+++ b/solution.py
@@ -152,8 +152,8 @@
         for n in range(1, xs):
             x_copy(n, part, c).start()
 
-    def send_attn():
-        for k in range(strips):
+    def send_attn(k_first, k_end):
+        for k in range(k_first, k_end):
             for i in range(1, ys):
                 attn_copy(i, k).start()
 
@@ -363,12 +363,6 @@
     def away(slot):
         return slot != z
 
-    def away_first(slot):
-        return (slot != z) & first
-
-    def away_plain(slot):
-        return (slot != z) & jnp.logical_not(first)
-
     def home(slot):
         return slot == z
 
@@ -380,6 +374,12 @@
 
     def far(slot):
         return (slot != z) & (slot // 2 != x)
+
+    def outer(slot):
+        return far(slot) & ((slot == 0) | (slot == zs - 1))
+
+    def inner(slot):
+        return far(slot) & (slot != 0) & (slot != zs - 1)
 
     def is_first(slot):
         return slot == beside
@@ -484,14 +484,21 @@
         def _():
             send_y(c)
 
+    pltpu.make_async_copy(attn.at[:, mine, :], attn.at[:, mine, :], attn_sem).wait()
+    send_attn(0, two)
+
     @pl.when(first)
     def _():
         for c in range(early, chunks):
             make_sent(c)
             send_y(c)
 
-    pltpu.make_async_copy(attn.at[:, mine, :], attn.at[:, mine, :], attn_sem).wait()
-    send_attn()
+    send_attn(two, strips - rest)
+
+    @pl.when(jnp.logical_not(plain))
+    def _():
+        send_attn(strips - rest, strips)
+
     for c in range(1, early):
         make_own(c)
     for load in loads[2:]:
@@ -519,10 +526,6 @@
         for c in range(early, chunks):
             make_own(c)
             send_x(y, c)
-            relay_y(c)
-
-    for c in range(1, early):
-        relay_x(y, c, away_first)
 
     attn_arrive(0)
     gather_partner(partner, 0, early, away)
@@ -530,9 +533,7 @@
     tick()
     coef_steps()
     for c in range(1, early):
-        relay_x(y, c, away_plain)
-        for part in parts[1:]:
-            relay_x(part, c, away_first)
+        relay_x(y, c, away)
     coef_steps()
     if two > 1:
         attn_arrive(1)
@@ -541,24 +542,14 @@
     coef_steps()
     for c in range(1, early):
         for part in parts[1:]:
-            relay_x(part, c, away_plain)
-    soon_left = list(soon_ids)
-    if rest:
-        gather_partner(partner, early, chunks, is_first)
-        run([soon_left[0]], near_first, never)
+            relay_x(part, c, away)
+    catch = min(two + 2, strips - 1)
     for other in others:
         gather_partner(other + 1 - core, 0, early, away)
     for k in range(two):
         run([k], far, far)
         tick()
     if rest:
-        for c in range(early, chunks):
-            for part in parts:
-                relay_x(part, c, is_first)
-        for other in others:
-            gather_partner(other + 1 - core, early, chunks, is_first)
-        run([soon_left.pop(0)], far_first, never)
-
         @pl.when(plain | last)
         def _():
             for c in range(early, chunks):
@@ -566,8 +557,9 @@
 
         @pl.when(plain)
         def _():
-            for c in range(early, chunks):
-                send_y(c)
+            for n in range(rest):
+                send_y(early + n)
+                send_attn(strips - rest + n, strips - rest + n + 1)
 
         @pl.when(plain | last)
         def _():
@@ -584,12 +576,50 @@
         for c in range(chunks):
             send_y(c)
 
+    def late_near(c, ms):
+        @pl.when(plain)
+        def _():
+            relay_y(c)
+
+        relay_x(y, c, is_plain)
+        gather_partner(partner, c, c + 1, is_plain)
+        run(ms, near_plain, near)
+
+    def late_far(c):
+        for part in parts[1:]:
+            relay_x(part, c, is_plain)
+        for other in others:
+            gather_partner(other + 1 - core, c, c + 1, is_plain)
+
     for k in range(two, strips):
+        n = k - (strips - rest)
+        if n >= 0:
+            late_near(early + n, late_of(early + n)[:1])
+        if n == 1:
+            late_far(early)
+            run(late_of(early)[:1], far_plain, far)
+        if k == two and rest:
+            @pl.when(first)
+            def _():
+                for c in range(early, chunks):
+                    relay_y(c)
+
         attn_arrive(k)
         run([k], away, away)
         tick()
-        if soon_left:
-            run([soon_left.pop(0)], is_first, never)
+        if rest:
+            have = soon_ids[: k - two + 2]
+            if k == two:
+                gather_partner(partner, early, chunks, is_first)
+            run(have if k == two else have[-1:], near_first, never)
+            if k == catch:
+                for c in range(early, chunks):
+                    for part in parts:
+                        relay_x(part, c, is_first)
+                for other in others:
+                    gather_partner(other + 1 - core, early, chunks, is_first)
+            if k >= catch:
+                run(have if k == catch else have[-1:], far_first, never)
         if k % 2:
             coef_steps()
         if k == two:
@@ -602,53 +632,37 @@
     coef_a[2] = coef_a[1]
     coef_partner(True)
 
-    for c in range(early, chunks):
-        relay_x(y, c, is_plain)
     for c in range(chunks):
         relay_x(y, c, home)
-    behind = list(range(chunks))
     started = len(queue)
-    for c in range(early, chunks):
-        @pl.when(plain)
-        def _():
+
+    @pl.when(last)
+    def _():
+        for c in range(chunks // 2):
             relay_y(c)
 
-        now, behind = behind[: -(-chunks // max(rest, 1))], behind[-(-chunks // max(rest, 1)):]
-
-        @pl.when(last)
-        def _():
-            for d in now:
-                relay_y(d)
-
-        gather_partner(partner, c, c + 1, is_plain)
-        run(late_of(c), near_plain, near)
-        advance(1, len(queue) - LAG)
+    if rest:
+        run([m for c in range(early, chunks) for m in late_of(c)[1:]], near_plain, near)
+        advance(1, started)
 
     @pl.when(last)
     def _():
-        for d in behind:
-            relay_y(d)
-
-    advance(2, started)
-
-    for c in range(early, chunks):
-        for part in parts[1:]:
-            relay_x(part, c, is_plain)
-        if c == early:
-            coef_partner(False)
-            coef_c[x] = coef_a[2] + coef_b[2]
-            for n in range(1, xs):
-                coef_x(n, x).start()
-        for other in others:
-            gather_partner(other + 1 - core, c, c + 1, is_plain)
-        run(late_of(c), far_plain, far)
-        advance(1, len(queue) - LAG)
-        advance(2, started + c - early)
-    if not rest:
-        coef_partner(False)
-        coef_c[x] = coef_a[2] + coef_b[2]
-        for n in range(1, xs):
-            coef_x(n, x).start()
+        for c in range(chunks // 2, chunks):
+            relay_y(c)
+
+    advance(2, started - 1)
+    coef_partner(False)
+    coef_c[x] = coef_a[2] + coef_b[2]
+    for n in range(1, xs):
+        coef_x(n, x).start()
+    if rest:
+        left = list(late_of(early)[1:])
+        for c in range(early + 1, chunks):
+            late_far(c)
+            left += late_of(c)
+        run(left, far_plain, outer)
+        queue.append((left, inner))
+        advance(1, len(queue))
     for n in range(1, xs):
         coef_x(n, (x + n) % xs).wait_recv()
     total = coef_c[0]

time: 120 us -> 115 us (0.958)
  Pallas kernels: 119 us -> 113 us
    pallas_call x1, Pallas kernels: 116 us -> 111 us  [local(): pl.pallas_call(functools.partial(kernel, dp_size, tensor_size), out_shape...]
where the time goes in v3:
time: 115 us; the launch traced here: 114 us
  Pallas kernels  113 us (98%)
    pallas_call x1, Pallas kernels, local(): pl.pallas_call(functools.partial(kernel, dp_size, tensor_size), out_shape...  111 us
    pallas_call x1, Pallas kernels, local(): pl.pallas_call(settle, grid=(2,), out_shape=(jax.ShapeDtypeStruct(dwa_coe...  2.63 us

profile of v3, /device:TPU:2, one launch (start us, length us, event | category | flops | bytes accessed | tf_op | source)
XLA Modules:
  0.0 114.1 jit_solution(18189447531613003571)
XLA Ops:
  0.6 110.8 %shard_map.59 = (f32[8,128]{1,0:T(8,128)}, f32[512,1024]{1,0:T(8,128)}) custom-call(bf16[5,1024,1024]{2,1,0:T(8,128)(2,1)} %outs_hbm.1, bf16[4,1024,1024]{2,1,0:T(8,128)(2,1)} %grads_hbm.1, bf16[1024,1024]{1,0:T(8,128)(2,1)} %attn_hbm.1, f32[4,5]{1,0:T(4,128)} %coefs.1), custom_call_target="tpu_custom_call" | custom-call | tf_op jit(solution)/shard_map/pallas_call | solution.py:789
  111.5 2.6 %shard_map.60 = (f32[4,5]{1,0:T(4,128)}, f32[512,1024]{1,0:T(8,128)}) custom-call(f32[8,128]{1,0:T(8,128)} %get-tuple-element.4.coef, f32[512,1024]{1,0:T(8,128)} %get-tuple-element.5.proj), custom_call_target="tpu_custom_call" | custom-call | tf_op jit(solution)/shard_map/pallas_call | solution.py:832

commit v4 on v3

--- a/solution.py
+++ b/solution.py
@@ -699,35 +699,61 @@
     coef_store = pltpu.make_async_copy(coef_b.at[2], coef_out, load_sem.at[0])
     coef_store.start()
 
-    @pl.when(z > 0)
-    def _():
+    def from_left():
         pltpu.make_async_remote_copy(
             src_ref=z_left.at[z], dst_ref=z_left.at[z],
             send_sem=z_send_sem.at[z], recv_sem=z_sem.at[zs * passing],
             device_id={"dp": dp - ys}, device_id_type=mesh_id,
         ).wait_recv()
 
-    @pl.when(z < zs - 1)
-    def _():
+    def from_right():
         pltpu.make_async_remote_copy(
             src_ref=z_right.at[z], dst_ref=z_right.at[z],
             send_sem=z_send_sem.at[z], recv_sem=z_sem.at[zs * passing + 1],
             device_id={"dp": dp + ys}, device_id_type=mesh_id,
         ).wait_recv()
 
+    low = z < zs // 2
+    high = jnp.logical_not(low)
+
+    @pl.when(low & (z > 0))
+    def _():
+        from_left()
+
+        @pl.loop(0, strips)
+        def _(k):
+            own[z, k] += z_left[z, k].astype(jnp.float32)
+
+    @pl.when(high & (z < zs - 1))
+    def _():
+        from_right()
+
+        @pl.loop(0, strips)
+        def _(k):
+            own[z, k] += z_right[z, k].astype(jnp.float32)
+
+    @pl.when(low)
+    def _():
+        from_right()
+
+    @pl.when(high)
+    def _():
+        from_left()
+
     for c in range(chunks):
         at = lane_rows(c)
-        for k in range(strips):
-            lanes = slice(k * LANES, (k + 1) * LANES)
-            result[at, lanes] = own[z, k, at, :]
-
-            @pl.when(z > 0)
-            def _():
-                result[at, lanes] += z_left[z, k, at, :].astype(jnp.float32)
-
-            @pl.when(z < zs - 1)
-            def _():
-                result[at, lanes] += z_right[z, k, at, :].astype(jnp.float32)
+
+        @pl.when(low)
+        def _():
+            for k in range(strips):
+                lanes = slice(k * LANES, (k + 1) * LANES)
+                result[at, lanes] = own[z, k, at, :] + z_right[z, k, at, :].astype(jnp.float32)
+
+        @pl.when(high)
+        def _():
+            for k in range(strips):
+                lanes = slice(k * LANES, (k + 1) * LANES)
+                result[at, lanes] = own[z, k, at, :] + z_left[z, k, at, :].astype(jnp.float32)
 
         pltpu.make_async_copy(result.at[at, :], proj_out.at[at, :], attn_sem).start()
 

time: 115 us -> 115 us (level)
  no operation moved by 1% of the time
where the time goes in v4:
time: 115 us; the launch traced here: 114 us
  Pallas kernels  113 us (98%)
    pallas_call x1, Pallas kernels, local(): pl.pallas_call(functools.partial(kernel, dp_size, tensor_size), out_shape...  111 us
    pallas_call x1, Pallas kernels, local(): pl.pallas_call(settle, grid=(2,), out_shape=(jax.ShapeDtypeStruct(dwa_coe...  2.63 us

profile of v4, /device:TPU:2, one launch (start us, length us, event | category | flops | bytes accessed | tf_op | source)
XLA Modules:
  0.0 113.9 jit_solution(12120765737805266632)
XLA Ops:
  0.6 110.6 %shard_map.59 = (f32[8,128]{1,0:T(8,128)}, f32[512,1024]{1,0:T(8,128)}) custom-call(bf16[5,1024,1024]{2,1,0:T(8,128)(2,1)} %outs_hbm.1, bf16[4,1024,1024]{2,1,0:T(8,128)(2,1)} %grads_hbm.1, bf16[1024,1024]{1,0:T(8,128)(2,1)} %attn_hbm.1, f32[4,5]{1,0:T(4,128)} %coefs.1), custom_call_target="tpu_custom_call" | custom-call | tf_op jit(solution)/shard_map/pallas_call | solution.py:815
  111.2 2.6 %shard_map.60 = (f32[4,5]{1,0:T(4,128)}, f32[512,1024]{1,0:T(8,128)}) custom-call(f32[8,128]{1,0:T(8,128)} %get-tuple-element.4.coef, f32[512,1024]{1,0:T(8,128)} %get-tuple-element.5.proj), custom_call_target="tpu_custom_call" | custom-call | tf_op jit(solution)/shard_map/pallas_call | solution.py:858
